TPU v7x, 32 devices: a whole 2x2x4 slice. The times are simulated.
32 devices in a mesh: gx: 4 (over y, x), gy: 2 (over core), gz: 4 (over z).
Axes of the slice: x: 2, y: 2, z: 4, core: 2. Of those that a mesh axis runs over, the one named last changes fastest.
Arguments:
- labels: int32 [128, 128, 512], P('gx', 'gy', 'gz'), may hold values from 0 to 7
- conductivity: float32 [7, 8], replicated, may hold values from -0.08 to 2, as said below
- right_side: float32 [128, 128, 512], P('gx', 'gy', 'gz'), may hold values from -18 to 18
Outputs:
- solution: float32 [128, 128, 512], P('gx', 'gy', 'gz')
Inputs may be any that keep to these rules, and one draw needn't show every extreme that they name: `conductivity`: rows 0 to 2 are positive, rows 3 to 5 have magnitude at most 0.08, row 6 is at least 0.5.
All inputs are finite; a program needn't handle non-finite values.
Results may differ from a plain program's by a relative error of at most 0.0001.
Values sent between devices are 32-bit elements; how exact they have to be, the bound alone decides.
A program may use at most 128 MiB of HBM per device.

v0:
```python
import jax
import jax.numpy as jnp
from jax import lax
from jax.sharding import PartitionSpec as P

ITERS = 3


def with_halo(cells, sides, width):
    for axis, dim in sides:
        count = lax.axis_size(axis)
        ends = count - 1
        head = lax.slice_in_dim(cells, 0, width, axis=dim)
        tail = lax.slice_in_dim(cells, cells.shape[dim] - width, cells.shape[dim], axis=dim)
        cells = jnp.concatenate(
            [
                lax.ppermute(tail, axis, [(i, (i + 1) % count) for i in range(ends)]),
                cells,
                lax.ppermute(head, axis, [((i + 1) % count, i) for i in range(ends)]),
            ],
            axis=dim,
        )
    return cells


def neighbour_value(arr, shift_x, shift_y, shift_z, cell_grid):
    size_x, size_y, size_z = cell_grid
    return arr[
        ...,
        1 + shift_x : 1 + shift_x + size_x,
        1 + shift_y : 1 + shift_y + size_y,
        1 + shift_z : 1 + shift_z + size_z,
    ]


def stencil_apply(padded_value, padded_sigma, self_coefficient):
    cell_grid = self_coefficient.shape
    value_entry = neighbour_value(padded_value, 0, 0, 0, cell_grid)
    total_flux = self_coefficient * value_entry
    for axis in range(3):
        for sign in (-1, 1):
            stencil_offset = [0, 0, 0]
            stencil_offset[axis] = sign
            face_flux = 0.5 * (
                neighbour_value(padded_sigma[axis], 0, 0, 0, cell_grid)
                + neighbour_value(
                    padded_sigma[axis],
                    stencil_offset[0],
                    stencil_offset[1],
                    stencil_offset[2],
                    cell_grid,
                )
            )
            total_flux = total_flux + face_flux * (
                value_entry
                - neighbour_value(
                    padded_value, stencil_offset[0], stencil_offset[1], stencil_offset[2], cell_grid
                )
            )
    for first, second, comp in ((0, 1, 3), (0, 2, 4), (1, 2, 5)):
        for sign_a in (-1, 1):
            for sign_b in (-1, 1):
                stencil_offset = [0, 0, 0]
                stencil_offset[first] = sign_a
                stencil_offset[second] = sign_b
                cross_term = (
                    0.25
                    * sign_a
                    * sign_b
                    * (
                        neighbour_value(padded_sigma[comp], 0, 0, 0, cell_grid)
                        + neighbour_value(
                            padded_sigma[comp],
                            stencil_offset[0],
                            stencil_offset[1],
                            stencil_offset[2],
                            cell_grid,
                        )
                    )
                )
                total_flux = total_flux - cross_term * neighbour_value(
                    padded_value, stencil_offset[0], stencil_offset[1], stencil_offset[2], cell_grid
                )
    return total_flux


def diagonal_of(padded_sigma, self_coefficient):
    cell_grid = self_coefficient.shape
    total_flux = self_coefficient
    for axis in range(3):
        for sign in (-1, 1):
            stencil_offset = [0, 0, 0]
            stencil_offset[axis] = sign
            total_flux = total_flux + 0.5 * (
                neighbour_value(padded_sigma[axis], 0, 0, 0, cell_grid)
                + neighbour_value(
                    padded_sigma[axis],
                    stencil_offset[0],
                    stencil_offset[1],
                    stencil_offset[2],
                    cell_grid,
                )
            )
    return total_flux


def lookup(shifted, conductivity):
    total_flux = jnp.zeros((7,) + shifted.shape, jnp.float32)
    for label in range(conductivity.shape[1]):
        hit = (shifted == label + 1).astype(jnp.float32)
        total_flux = total_flux + hit[None] * conductivity[:, label][:, None, None, None]
    return total_flux


def apply_operator(field, padded_sigma, self_coefficient):
    field_pad = with_halo(field, (("gx", 0), ("gy", 1), ("gz", 2)), 1)
    return stencil_apply(field_pad, padded_sigma, self_coefficient)


def local(labels, conductivity, right_side):
    shifted = labels + 1
    own_table = lookup(shifted, conductivity)
    padded_sigma = with_halo(own_table[:6], (("gx", 1), ("gy", 2), ("gz", 3)), 1)
    self_coefficient = own_table[6]
    diag = diagonal_of(padded_sigma, self_coefficient)
    solution = jnp.zeros_like(right_side)
    residual = right_side
    precond = residual / diag
    applied = apply_operator(precond, padded_sigma, self_coefficient)
    gamma_old = jnp.float32(1.0)
    alpha_old = jnp.float32(1.0)
    direction = precond
    for step in range(ITERS):
        gamma, delta = lax.psum(
            (jnp.sum(residual * precond), jnp.sum(applied * precond)), ("gx", "gy", "gz")
        )
        if step + 1 < ITERS:
            scaled = applied / diag
            product = apply_operator(scaled, padded_sigma, self_coefficient)
        if step == 0:
            alpha = gamma / delta
            direction = precond
            along_z = product
            along_q = scaled
            along_s = applied
        else:
            ratio = gamma / gamma_old
            alpha = gamma / (delta - ratio * gamma / alpha_old)
            direction = precond + ratio * direction
            if step + 1 < ITERS:
                along_z = product + ratio * along_z
                along_q = scaled + ratio * along_q
                along_s = applied + ratio * along_s
        solution = solution + alpha * direction
        if step + 1 < ITERS:
            residual = residual - alpha * along_s
            precond = precond - alpha * along_q
            applied = applied - alpha * along_z
        gamma_old = gamma
        alpha_old = alpha
    return solution


def solution(mesh):
    return jax.shard_map(
        local,
        mesh=mesh,
        in_specs=(P("gx", "gy", "gz"), P(), P("gx", "gy", "gz")),
        out_specs=P("gx", "gy", "gz"),
        check_vma=False,
    )
```

profile of v0, /device:TPU:0, one launch (start us, length us, event | category | flops | bytes accessed | tf_op | source)
XLA Modules:
  0.0 398.3 jit_solution(9120328655755178801)
XLA Ops:
  3.6 4.1 %multiply_add_fusion = f32[7,32,64,128]{3,2,1,0:T(8,128)S(1)} fusion(f32[7]{0:T(128)S(1)} %get-tuple-element.15, f32[32,64,128]{2,1,0:T(8,128)S(1)} %get-tuple-element.83, f32[7]{0:T(128)S(1)} %get-tuple-element.16, f32[32,64,128]{2,1,0:T(8,128)S(1)} %get-tuple-element.82, f32[7]{0:T(128)S(1)} %get-tuple-element.10, f32[32,64,128]{2,1,0:T(8,128)S(1)} %get-tuple-element.81, ...), kind=kLoop, calls=%fused_computation.2 | loop fusion | flops 27525120 | bytes 15728864 | tf_op jit(solution)/shard_map/add | solution.py:111
  7.8 4.9 %collective-permute-start = (f32[6,1,64,128]{3,2,1,0:T(8,128)S(1)}, f32[6,1,64,128]{3,2,1,0:T(8,128)S(1)}, u32[]{:S(2)}, u32[]{:S(2)}) collective-permute-start(f32[6,1,64,128]{3,2,1,0:T(8,128)S(1)} %get-tuple-element.42), channel_id=1, source_target_pairs={{0,8},{8,16},{16,24},{1,9},{9,17},{17,25},{2,10},{10,18},{18,26},{... | collective-permute-start | bytes 589832 | tf_op jit(solution)/shard_map/ppermute | solution.py:17
  16.8 6.2 %collective-permute-done.1 = f32[6,1,64,128]{3,2,1,0:T(8,128)S(1)} collective-permute-done((f32[6,1,64,128]{3,2,1,0:T(8,128)S(1)}, f32[6,1,64,128]{3,2,1,0:T(8,128)S(1)}, u32[]{:S(2)}, u32[]{:S(2)}) %collective-permute-start.1) | collective-permute-done | bytes 196640 | tf_op jit(solution)/shard_map/ppermute | solution.py:19
  31.2 12.6 %fusion.111 = (f32[6,34,66,1]{3,2,1,0:T(8,128)}, f32[6,34,66,1]{3,2,1,0:T(8,128)}) fusion(f32[6,34,66,128]{3,2,1,0:T(8,128)} %pad_maximum_fusion.1), kind=kLoop, calls=%fused_computation.239 | loop fusion | bytes 215424 | tf_op jit(solution)/shard_map/slice | solution.py:14
  43.8 5.1 %copy.16 = f32[6,34,66,1]{2,3,1,0:T(1,128)S(1)} copy(f32[6,34,66,1]{3,2,1,0:T(8,128)} %get-tuple-element.40) | data formatting | bytes 107712 | tf_op jit(solution)/shard_map/slice | solution.py:14
  52.4 5.1 %copy.17 = f32[6,34,66,1]{2,3,1,0:T(1,128)S(1)} copy(f32[6,34,66,1]{3,2,1,0:T(8,128)} %get-tuple-element.41) | data formatting | bytes 107712 | tf_op jit(solution)/shard_map/slice | solution.py:13
  59.0 4.9 %copy.18 = f32[6,34,66,1]{3,2,1,0:T(8,128)} copy(f32[6,34,66,1]{2,3,1,0:T(1,128)S(1)} %collective-permute-done.4) | data formatting | bytes 107712 | tf_op jit(solution)/shard_map/ppermute | solution.py:17
  64.1 4.7 %copy.19 = f32[6,34,66,1]{3,2,1,0:T(8,128)} copy(f32[6,34,66,1]{2,3,1,0:T(1,128)S(1)} %collective-permute-done.5) | data formatting | bytes 107712 | tf_op jit(solution)/shard_map/ppermute | solution.py:19
  68.7 18.9 %pad_maximum_fusion = f32[6,34,66,130]{3,2,1,0:T(8,128)} fusion(f32[6,34,66,1]{3,2,1,0:T(8,128)} %copy.19, f32[6,34,1,128]{3,2,1,0:T(1,128)S(1)} %collective-permute-done.3, f32[6,1,64,128]{3,2,1,0:T(8,128)S(1)} %collective-permute-done.1, f32[6,32,64,128]{3,2,1,0:T(8,128)} %copy-done.9, f32[6,1,64,128]{3,2,1,0:T(8,128)S(1)} %collective-permute-done, ...), kind=kLoop, calls=%fused_computation | loop fusion | flops 10501920 | bytes 14002560 | tf_op jit(solution)/shard_map/concatenate | solution.py:15
  87.6 10.2 %slice_bitcast_fusion.2 = (f32[34,66,130]{2,1,0:T(8,128)S(1)}, f32[34,66,130]{2,1,0:T(8,128)}, f32[34,66,130]{2,1,0:T(8,128)}, f32[34,66,130]{2,1,0:T(8,128)}, f...) fusion(f32[6,34,66,130]{3,2,1,0:T(8,128)} %pad_maximum_fusion), kind=kLoop, calls=%fused_computation.5 | loop fusion | bytes 14002560 | tf_op jit(solution)/shard_map/squeeze | solution.py:71
  97.8 13.2 %fusion.104 = (f32[32,64,128]{2,1,0:T(8,128)S(1)}, f32[32,64,128]{2,1,0:T(8,128)}, f32[32,64,128]{2,1,0:T(8,128)}, f32[32,64,128]{2,1,0:T(8,128)}, f32[32,64,128...) fusion(f32[32,64,128]{2,1,0:T(8,128)} %param.5, ...), kind=kLoop, calls=%fused_computation.238 | loop fusion | flops 4980736 | bytes 19922944 | tf_op jit(solution)/shard_map/div | solution.py:128
  116.0 4.2 %collective-permute-done.7 = f32[1,64,128]{2,1,0:T(8,128)S(1)} collective-permute-done((f32[1,64,128]{2,1,0:T(8,128)S(1)}, f32[1,64,128]{2,1,0:T(8,128)S(1)}, u32[]{:S(2)}, u32[]{:S(2)}) %collective-permute-start.7) | collective-permute-done | bytes 32800 | tf_op jit(solution)/shard_map/ppermute | solution.py:19
  133.3 5.6 %collective-permute-start.10 = (f32[34,66,1]{1,2,0:T(1,128)}, f32[34,66,1]{1,2,0:T(1,128)}, u32[]{:S(2)}, u32[]{:S(2)}) collective-permute-start(f32[34,66,1]{1,2,0:T(1,128)} %copy.20), channel_id=1, source_target_pairs={{0,1},{1,2},{2,3},{4,5},{5,6},{6,7},{8,9},{9,10},{10,11},{12,13},{... | collective-permute-start | bytes 26936 | tf_op jit(solution)/shard_map/ppermute | solution.py:17
  150.2 9.8 %multiply_reduce_fusion.3 = (f32[]{:T(128)}, f32[]{:T(128)}, f32[32,64,128]{2,1,0:T(8,128)S(1)}) fusion(f32[32,64,128]{2,1,0:T(8,128)S(1)} %get-tuple-element.26, f32[32,64,128]{2,1,0:T(8,128)} %param.5, f32[34,66,129]{2,1,0:T(8,128)S(1)} %get-tuple-element.57, f32[34,66,130]{2,1,0:T(8,128)S(1)} %copy-done, f32[34,66,129]{2,1,0:T(8,128)S(1)} %get-tuple-element.56, ...), kind=kLoop, calls=%fused_computation.206 | loop fusion | flops 19136512 | bytes 43057160 | tf_op jit(solution)/shard_map/reduce_sum | solution.py:135
  164.6 4.2 %collective-permute-done.13 = f32[1,64,128]{2,1,0:T(8,128)S(1)} collective-permute-done((f32[1,64,128]{2,1,0:T(8,128)S(1)}, f32[1,64,128]{2,1,0:T(8,128)S(1)}, u32[]{:S(2)}, u32[]{:S(2)}) %collective-permute-start.13) | collective-permute-done | bytes 32800 | tf_op jit(solution)/shard_map/ppermute | solution.py:19
  172.6 40.9 %all-reduce.2 = (f32[]{:T(128)}, f32[]{:T(128)}) all-reduce(f32[]{:T(128)} %get-tuple-element.8, f32[]{:T(128)} %get-tuple-element.7), channel_id=1, replica_groups=mesh['gx'=4,'gy'=2,'gz'=4] {'gx','gy','gz'}, use_global_device_ids=true, to_apply=%region_1.0 | all-reduce | flops 2 | bytes 16 | tf_op jit(solution)/shard_map/psum | solution.py:134
  224.1 5.1 %collective-permute-start.16 = (f32[34,66,1]{1,2,0:T(1,128)}, f32[34,66,1]{1,2,0:T(1,128)}, u32[]{:S(2)}, u32[]{:S(2)}) collective-permute-start(f32[34,66,1]{1,2,0:T(1,128)} %copy.24), channel_id=1, source_target_pairs={{0,1},{1,2},{2,3},{4,5},{5,6},{6,7},{8,9},{9,10},{10,11},{12,13},{... | collective-permute-start | bytes 26936 | tf_op jit(solution)/shard_map/ppermute | solution.py:17
  242.0 9.4 %fusion.101 = (f32[32,64,128]{2,1,0:T(8,128)S(1)}, f32[32,64,128]{2,1,0:T(8,128)S(1)}) fusion(f32[32,64,128]{2,1,0:T(8,128)S(1)} %copy-done.18, f32[32,64,128]{2,1,0:T(8,128)S(1)} %copy-done.11, f32[]{:T(128)S(6)} %div.31, f32[34,66,129]{2,1,0:T(8,128)S(1)} %get-tuple-element.55, f32[34,66,130]{2,1,0:T(8,128)S(1)} %copy-done.1, ...), kind=kLoop, calls=%fused_computation.217 | loop fusion | flops 18874368 | bytes 45154308 | tf_op jit(solution)/shard_map/div | solution.py:138
  252.2 4.8 %collective-permute-start.18 = (f32[1,64,128]{2,1,0:T(8,128)}, f32[1,64,128]{2,1,0:T(8,128)}, u32[]{:S(2)}, u32[]{:S(2)}) collective-permute-start(f32[1,64,128]{2,1,0:T(8,128)} %get-tuple-element.70), channel_id=1, source_target_pairs={{0,8},{8,16},{16,24},{1,9},{9,17},{17,25},{2,10},{10,18},{18,26},{... | collective-permute-start | bytes 98312 | tf_op jit(solution)/shard_map/ppermute | solution.py:17
  259.5 41.2 %all-reduce.1 = (f32[]{:T(128)}, f32[]{:T(128)}) all-reduce(f32[]{:T(128)} %get-tuple-element.6, f32[]{:T(128)} %get-tuple-element.5), channel_id=1, replica_groups=mesh['gx'=4,'gy'=2,'gz'=4] {'gx','gy','gz'}, use_global_device_ids=true, to_apply=%region_5.0 | all-reduce | flops 2 | bytes 16 | tf_op jit(solution)/shard_map/psum | solution.py:134
  321.7 5.1 %collective-permute-start.22 = (f32[34,66,1]{1,2,0:T(1,128)}, f32[34,66,1]{1,2,0:T(1,128)}, u32[]{:S(2)}, u32[]{:S(2)}) collective-permute-start(f32[34,66,1]{1,2,0:T(1,128)} %copy.28), channel_id=1, source_target_pairs={{0,1},{1,2},{2,3},{4,5},{5,6},{6,7},{8,9},{9,10},{10,11},{12,13},{... | collective-permute-start | bytes 26936 | tf_op jit(solution)/shard_map/ppermute | solution.py:17
  334.8 4.1 %maximum_maximum_fusion.2 = (f32[34,66,129]{2,1,0:T(8,128)S(1)}, f32[34,66,129]{2,1,0:T(8,128)S(1)}) fusion(f32[34,1,128]{2,1,0:T(1,128)} %copy-done.34, f32[1,64,128]{2,1,0:T(8,128)} %collective-permute-done.19, f32[32,64,128]{2,1,0:T(8,128)} %copy-done.14, f32[1,64,128]{2,1,0:T(8,128)} %collective-permute-done.18, f32[34,1,128]{2,1,0:T(1,128)} %copy-done.32, ...), kind=kLoop, calls=%fused_computation.13 | loop fusion | flops 2894760 | bytes 3482688 | tf_op jit(solution)/shard_map/concatenate | solution.py:15
  339.6 10.8 %fusion.5 = f32[]{:T(128)} fusion(f32[34,66,129]{2,1,0:T(8,128)S(1)} %get-tuple-element.53, f32[34,66,129]{2,1,0:T(8,128)S(1)} %get-tuple-element.52, f32[34,65,128]{2,1,0:T(8,128)} %get-tuple-element.59, f32[34,65,128]{2,1,0:T(8,128)} %get-tuple-element.58, f32[32,64,128]{2,1,0:T(8,128)} %get-tuple-element.33, f32[32,64,128]{2,1,0:T(8,128)S(1)} %copy-done.16, ...), kind=kLoop, calls=%fused_computation.30 | loop fusion | flops 22020096 | bytes 46202896 | tf_op jit(solution)/shard_map/reduce_sum | solution.py:135
  350.3 40.4 %all-reduce = (f32[]{:T(128)}, f32[]{:T(128)}) all-reduce(f32[]{:T(128)} %multiply_reduce_fusion, f32[]{:T(128)} %fusion.5), channel_id=1, replica_groups=mesh['gx'=4,'gy'=2,'gz'=4] {'gx','gy','gz'}, use_global_device_ids=true, to_apply=%region_9.0 | all-reduce | flops 2 | bytes 16 | tf_op jit(solution)/shard_map/psum | solution.py:134
  (151 shorter events, 112.8 us)
Async XLA Ops:
  7.8 9.0 %collective-permute-start = (f32[6,1,64,128]{3,2,1,0:T(8,128)S(1)}, f32[6,1,64,128]{3,2,1,0:T(8,128)S(1)}, u32[]{:S(2)}, u32[]{:S(2)}) collective-permute-start(f32[6,1,64,128]{3,2,1,0:T(8,128)S(1)} %get-tuple-element.42), channel_id=1, source_target_pairs={{0,8},{8,16},{16,24},{1,9},{9,17},{17,25},{2,10},{10,18},{18,26},{... | collective-permute-start | bytes 589832 | tf_op jit(solution)/shard_map/ppermute | solution.py:17
  12.7 10.3 %collective-permute-start.1 = (f32[6,1,64,128]{3,2,1,0:T(8,128)S(1)}, f32[6,1,64,128]{3,2,1,0:T(8,128)S(1)}, u32[]{:S(2)}, u32[]{:S(2)}) collective-permute-start(f32[6,1,64,128]{3,2,1,0:T(8,128)S(1)} %get-tuple-element.43), channel_id=1, source_target_pairs={{8,0},{16,8},{24,16},{9,1},{17,9},{25,17},{10,2},{18,10},{26,18},{... | collective-permute-start | bytes 589832 | tf_op jit(solution)/shard_map/ppermute | solution.py:19
  23.1 2.6 collective-permute-start.2
  24.4 3.2 collective-permute-start.3
  48.9 10.1 %collective-permute-start.4 = (f32[6,34,66,1]{2,3,1,0:T(1,128)S(1)}, f32[6,34,66,1]{2,3,1,0:T(1,128)S(1)}, u32[]{:S(2)}, u32[]{:S(2)}) collective-permute-start(f32[6,34,66,1]{2,3,1,0:T(1,128)S(1)} %copy.16), channel_id=1, source_target_pairs={{0,1},{1,2},{2,3},{4,5},{5,6},{6,7},{8,9},{9,10},{10,11},{12,13},{... | collective-permute-start | bytes 161576 | tf_op jit(solution)/shard_map/ppermute | solution.py:17
  57.5 6.6 %collective-permute-start.5 = (f32[6,34,66,1]{2,3,1,0:T(1,128)S(1)}, f32[6,34,66,1]{2,3,1,0:T(1,128)S(1)}, u32[]{:S(2)}, u32[]{:S(2)}) collective-permute-start(f32[6,34,66,1]{2,3,1,0:T(1,128)S(1)} %copy.17), channel_id=1, source_target_pairs={{1,0},{2,1},{3,2},{5,4},{6,5},{7,6},{9,8},{10,9},{11,10},{13,12},{... | collective-permute-start | bytes 161576 | tf_op jit(solution)/shard_map/ppermute | solution.py:19
  111.0 5.0 %collective-permute-start.6 = (f32[1,64,128]{2,1,0:T(8,128)S(1)}, f32[1,64,128]{2,1,0:T(8,128)S(1)}, u32[]{:S(2)}, u32[]{:S(2)}) collective-permute-start(f32[1,64,128]{2,1,0:T(8,128)S(1)} %get-tuple-element.74), channel_id=1, source_target_pairs={{0,8},{8,16},{16,24},{1,9},{9,17},{17,25},{2,10},{10,18},{18,26},{... | collective-permute-start | bytes 98312 | tf_op jit(solution)/shard_map/ppermute | solution.py:17
  114.4 5.8 %collective-permute-start.7 = (f32[1,64,128]{2,1,0:T(8,128)S(1)}, f32[1,64,128]{2,1,0:T(8,128)S(1)}, u32[]{:S(2)}, u32[]{:S(2)}) collective-permute-start(f32[1,64,128]{2,1,0:T(8,128)S(1)} %get-tuple-element.75), channel_id=1, source_target_pairs={{8,0},{16,8},{24,16},{9,1},{17,9},{25,17},{10,2},{18,10},{26,18},{... | collective-permute-start | bytes 98312 | tf_op jit(solution)/shard_map/ppermute | solution.py:19
  120.3 2.6 collective-permute-start.8
  121.6 3.1 collective-permute-start.9
  132.0 11.6 %collective-permute-start.11 = (f32[34,66,1]{1,2,0:T(1,128)}, f32[34,66,1]{1,2,0:T(1,128)}, u32[]{:S(2)}, u32[]{:S(2)}) collective-permute-start(f32[34,66,1]{1,2,0:T(1,128)} %copy.22), channel_id=1, source_target_pairs={{1,0},{2,1},{3,2},{5,4},{6,5},{7,6},{9,8},{10,9},{11,10},{13,12},{... | collective-permute-start | bytes 26936 | tf_op jit(solution)/shard_map/ppermute | solution.py:19
  133.3 8.0 %collective-permute-start.10 = (f32[34,66,1]{1,2,0:T(1,128)}, f32[34,66,1]{1,2,0:T(1,128)}, u32[]{:S(2)}, u32[]{:S(2)}) collective-permute-start(f32[34,66,1]{1,2,0:T(1,128)} %copy.20), channel_id=1, source_target_pairs={{0,1},{1,2},{2,3},{4,5},{5,6},{6,7},{8,9},{9,10},{10,11},{12,13},{... | collective-permute-start | bytes 26936 | tf_op jit(solution)/shard_map/ppermute | solution.py:17
  160.2 4.4 %collective-permute-start.12 = (f32[1,64,128]{2,1,0:T(8,128)S(1)}, f32[1,64,128]{2,1,0:T(8,128)S(1)}, u32[]{:S(2)}, u32[]{:S(2)}) collective-permute-start(f32[1,64,128]{2,1,0:T(8,128)S(1)} %get-tuple-element.72), channel_id=1, source_target_pairs={{0,8},{8,16},{16,24},{1,9},{9,17},{17,25},{2,10},{10,18},{18,26},{... | collective-permute-start | bytes 98312 | tf_op jit(solution)/shard_map/ppermute | solution.py:17
  163.0 5.8 %collective-permute-start.13 = (f32[1,64,128]{2,1,0:T(8,128)S(1)}, f32[1,64,128]{2,1,0:T(8,128)S(1)}, u32[]{:S(2)}, u32[]{:S(2)}) collective-permute-start(f32[1,64,128]{2,1,0:T(8,128)S(1)} %get-tuple-element.73), channel_id=1, source_target_pairs={{8,0},{16,8},{24,16},{9,1},{17,9},{25,17},{10,2},{18,10},{26,18},{... | collective-permute-start | bytes 98312 | tf_op jit(solution)/shard_map/ppermute | solution.py:19
  169.4 45.5 %collective-permute-start.14 = (f32[34,1,128]{2,1,0:T(1,128)}, f32[34,1,128]{2,1,0:T(1,128)}, u32[]{:S(2)}, u32[]{:S(2)}) collective-permute-start(f32[34,1,128]{2,1,0:T(1,128)} %get-tuple-element.64), channel_id=1, source_target_pairs={{0,4},{1,5},{2,6},{3,7},{8,12},{9,13},{10,14},{11,15},{16,20},{17,... | collective-permute-start | bytes 52232 | tf_op jit(solution)/shard_map/ppermute | solution.py:17
  171.3 43.6 %collective-permute-start.15 = (f32[34,1,128]{2,1,0:T(1,128)}, f32[34,1,128]{2,1,0:T(1,128)}, u32[]{:S(2)}, u32[]{:S(2)}) collective-permute-start(f32[34,1,128]{2,1,0:T(1,128)} %get-tuple-element.65), channel_id=1, source_target_pairs={{4,0},{5,1},{6,2},{7,3},{12,8},{13,9},{14,10},{15,11},{20,16},{21,... | collective-permute-start | bytes 52232 | tf_op jit(solution)/shard_map/ppermute | solution.py:19
  222.9 12.0 %collective-permute-start.17 = (f32[34,66,1]{1,2,0:T(1,128)}, f32[34,66,1]{1,2,0:T(1,128)}, u32[]{:S(2)}, u32[]{:S(2)}) collective-permute-start(f32[34,66,1]{1,2,0:T(1,128)} %copy.26), channel_id=1, source_target_pairs={{1,0},{2,1},{3,2},{5,4},{6,5},{7,6},{9,8},{10,9},{11,10},{13,12},{... | collective-permute-start | bytes 26936 | tf_op jit(solution)/shard_map/ppermute | solution.py:19
  224.1 8.4 %collective-permute-start.16 = (f32[34,66,1]{1,2,0:T(1,128)}, f32[34,66,1]{1,2,0:T(1,128)}, u32[]{:S(2)}, u32[]{:S(2)}) collective-permute-start(f32[34,66,1]{1,2,0:T(1,128)} %copy.24), channel_id=1, source_target_pairs={{0,1},{1,2},{2,3},{4,5},{5,6},{6,7},{8,9},{9,10},{10,11},{12,13},{... | collective-permute-start | bytes 26936 | tf_op jit(solution)/shard_map/ppermute | solution.py:17
  252.2 52.9 %collective-permute-start.18 = (f32[1,64,128]{2,1,0:T(8,128)}, f32[1,64,128]{2,1,0:T(8,128)}, u32[]{:S(2)}, u32[]{:S(2)}) collective-permute-start(f32[1,64,128]{2,1,0:T(8,128)} %get-tuple-element.70), channel_id=1, source_target_pairs={{0,8},{8,16},{16,24},{1,9},{9,17},{17,25},{2,10},{10,18},{18,26},{... | collective-permute-start | bytes 98312 | tf_op jit(solution)/shard_map/ppermute | solution.py:17
  257.0 48.2 %collective-permute-start.19 = (f32[1,64,128]{2,1,0:T(8,128)}, f32[1,64,128]{2,1,0:T(8,128)}, u32[]{:S(2)}, u32[]{:S(2)}) collective-permute-start(f32[1,64,128]{2,1,0:T(8,128)} %get-tuple-element.71), channel_id=1, source_target_pairs={{8,0},{16,8},{24,16},{9,1},{17,9},{25,17},{10,2},{18,10},{26,18},{... | collective-permute-start | bytes 98312 | tf_op jit(solution)/shard_map/ppermute | solution.py:19
  306.1 6.8 %collective-permute-start.20 = (f32[34,1,128]{2,1,0:T(1,128)S(1)}, f32[34,1,128]{2,1,0:T(1,128)S(1)}, u32[]{:S(2)}, u32[]{:S(2)}) collective-permute-start(f32[34,1,128]{2,1,0:T(1,128)S(1)} %get-tuple-element.60), channel_id=1, source_target_pairs={{0,4},{1,5},{2,6},{3,7},{8,12},{9,13},{10,14},{11,15},{16,20},{17,... | collective-permute-start | bytes 52232 | tf_op jit(solution)/shard_map/ppermute | solution.py:17
  307.4 5.5 %collective-permute-start.21 = (f32[34,1,128]{2,1,0:T(1,128)S(1)}, f32[34,1,128]{2,1,0:T(1,128)S(1)}, u32[]{:S(2)}, u32[]{:S(2)}) collective-permute-start(f32[34,1,128]{2,1,0:T(1,128)S(1)} %get-tuple-element.61), channel_id=1, source_target_pairs={{4,0},{5,1},{6,2},{7,3},{12,8},{13,9},{14,10},{15,11},{20,16},{21,... | collective-permute-start | bytes 52232 | tf_op jit(solution)/shard_map/ppermute | solution.py:19
  320.4 12.0 %collective-permute-start.23 = (f32[34,66,1]{1,2,0:T(1,128)}, f32[34,66,1]{1,2,0:T(1,128)}, u32[]{:S(2)}, u32[]{:S(2)}) collective-permute-start(f32[34,66,1]{1,2,0:T(1,128)} %copy.30), channel_id=1, source_target_pairs={{1,0},{2,1},{3,2},{5,4},{6,5},{7,6},{9,8},{10,9},{11,10},{13,12},{... | collective-permute-start | bytes 26936 | tf_op jit(solution)/shard_map/ppermute | solution.py:19
  321.7 8.4 %collective-permute-start.22 = (f32[34,66,1]{1,2,0:T(1,128)}, f32[34,66,1]{1,2,0:T(1,128)}, u32[]{:S(2)}, u32[]{:S(2)}) collective-permute-start(f32[34,66,1]{1,2,0:T(1,128)} %copy.28), channel_id=1, source_target_pairs={{0,1},{1,2},{2,3},{4,5},{5,6},{6,7},{8,9},{9,10},{10,11},{12,13},{... | collective-permute-start | bytes 26936 | tf_op jit(solution)/shard_map/ppermute | solution.py:17
  (36 other events, 195.0 us)
where the time goes:
time: 400 us; the launch traced here: 398 us
  blocking collectives  123 us (31%)
  other arithmetic  106 us (26%)
  local copies, waits for them, and re-layouts  81.7 us (20%)
  starting transfers between devices  57 us (14%)
  waiting for transfers between devices  20.8 us (5%)
  between operations  10.1 us (3%)
    psum x3, blocking collectives, local(): lax.psum((jnp.sum(residual * precond), jnp.sum(applied * precond)), ('gx'...  123 us
    concatenate x11, other arithmetic, with_halo(): jnp.concatenate([lax.ppermute(tail, axis, [(i, (i + 1) % count) for i in...  45.8 us
    ppermute x12, starting transfers between devices, with_halo(): lax.ppermute(tail, axis, [(i, (i + 1) % count) for i in range(ends)])  41 us
    slice x12, local copies, waits for them, and re-layouts, with_halo(): lax.slice_in_dim(cells, cells.shape[dim] - width, cells.shape[dim], axis=...  31 us
    reduce_sum x3, other arithmetic, local(): jnp.sum(applied * precond)  21.8 us
    ppermute x12, waiting for transfers between devices, with_halo(): lax.ppermute(head, axis, [((i + 1) % count, i) for i in range(ends)])  18.5 us
    ppermute x12, starting transfers between devices, with_halo(): lax.ppermute(head, axis, [((i + 1) % count, i) for i in range(ends)])  16 us
    div x1, other arithmetic, local(): precond = residual / diag  13.2 us
  transfers between devices with their start and end apart: 24, of which 9 were waited for; matrix products, arithmetic and copies ran while one was open for 8% of the time, Pallas kernels for 0%

commit v1 on v0

v1 whole, which is shorter than its diff:
```python
import functools
import jax
import jax.numpy as jnp
from jax import lax
from jax.experimental import pallas as pl
from jax.experimental.pallas import tpu as pltpu
from jax.sharding import PartitionSpec as P

ITERS = 3
AXES = ("gx", "gy", "gz")
ROUNDS = ITERS + 1
MOMENTS = 2 * ITERS
LANES = 128
PAD = 8
CH = 16


def kernel(
    sizes, lab, cond, rhs, out, V, S, DI, PS, PR, ES, ER, HB, HS, PG, CP, MA, RS, RR,
    send_sem, recv_sem, ar_send, ar_recv,
):
    X, Y, Z = rhs.shape
    YE = Y + 2 * PAD
    TOP = PAD + Y
    me = [lax.axis_index(a) for a in AXES]
    f32 = jnp.float32

    directions = []
    for dx in (-1, 0, 1):
        for dy in (-1, 0, 1):
            for dz in (-1, 0, 1):
                d = (dx, dy, dz)
                live = sum(1 for t in d if t)
                if live in (1, 2) and all(n > 1 for t, n in zip(d, sizes) if t):
                    directions.append(d)

    def present(d):
        ok = None
        for t, m, n in zip(d, me, sizes):
            if t == 0:
                continue
            here = (m < n - 1) if t > 0 else (m > 0)
            ok = here if ok is None else jnp.logical_and(ok, here)
        return ok

    def places(d, r):
        dx, dy, dz = d
        rows_from = pl.ds(PAD, Y) if dy == 0 else (pl.ds(TOP - 8, 8) if dy > 0 else pl.ds(PAD, 8))
        rows_to = pl.ds(PAD, Y) if dy == 0 else (pl.ds(0, 8) if dy > 0 else pl.ds(TOP, 8))
        if dz == 0:
            if dx == 0:
                return V.at[r, pl.ds(1, X), rows_from], V.at[r, pl.ds(1, X), rows_to]
            fx, tx = (X, 0) if dx > 0 else (1, X + 1)
            return V.at[r, fx, rows_from], V.at[r, tx, rows_to]
        side = 0 if dz > 0 else 1
        if dx == 0:
            return PS.at[r, rows_from], PR.at[r, side, rows_to]
        slot = (0 if dx > 0 else 2) + side
        return ES.at[r], ER.at[r, slot]

    def copy(d, r):
        src, dst = places(d, r)
        m = directions.index(d)
        return pltpu.make_async_remote_copy(
            src_ref=src,
            dst_ref=dst,
            send_sem=send_sem.at[r, m],
            recv_sem=recv_sem.at[r, m],
            device_id=tuple(a + t for a, t in zip(me, d)),
            device_id_type=pl.DeviceIdType.MESH,
        )

    for d in [
        (dx, dy, dz)
        for dx in (-1, 0, 1)
        for dy in (-1, 0, 1)
        for dz in (-1, 0, 1)
        if sum(1 for t in (dx, dy, dz) if t) in (1, 2)
    ]:
        def clear(d=d):
            for r in range(ROUNDS):
                _, dst = places(d, r)
                dst[...] = jnp.zeros(dst.shape, f32)

        if d in directions:
            back = tuple(-t for t in d)
            pl.when(jnp.logical_not(present(back)))(clear)
        else:
            clear()

    def start(r):
        lane8 = lax.broadcasted_iota(jnp.int32, (8, LANES), 1)
        tile = jnp.zeros((8, LANES), f32)
        for col, at in enumerate((0, LANES - 1, 2 * (X - 1), 2 * (X - 1) - 1)):
            for k in range(Y // 8):
                to = col * (Y // 8) + k
                part = PS[r, pl.ds(PAD + 8 * k, 8), :]
                tile = jnp.where(lane8 == to, pltpu.roll(part, (to - at) % LANES, 1), tile)
        ES[r] = tile
        for d in directions:
            pl.when(present(d))(lambda d=d: copy(d, r).start())

    def wait(r):
        for d in directions:
            back = tuple(-t for t in d)
            pl.when(present(back))(lambda d=d: copy(d, r).wait_recv())

    lane_e = lax.broadcasted_iota(jnp.int32, (YE, LANES), 1)
    lane_c = lax.broadcasted_iota(jnp.int32, (CH, LANES), 1)
    lane_8 = lax.broadcasted_iota(jnp.int32, (8, LANES), 1)
    even = lane_e % 2 == 0
    lane_y = lax.broadcasted_iota(jnp.int32, (Y, LANES), 1)

    def build_halo(r):
        low = pltpu.roll(PR[r, 0], 1, 1)
        high = pltpu.roll(PR[r, 1], LANES - 1, 1)
        valid = jnp.logical_or(lane_e <= 2 * (X - 1), lane_e == LANES - 1)
        HB[...] = jnp.where(valid, jnp.where(even, low, high), 0.0)
        targets = (((LANES - 2), 3), ((LANES - 3), 2), (2 * X, 1), (2 * X - 1, 0))
        tiles = [ER[r, slot] for slot in range(4)]
        for k in range(Y // 8):
            rows = pl.ds(PAD + 8 * k, 8)
            part = HB[rows, :]
            for slot, (target, col) in enumerate(targets):
                at = col * (Y // 8) + k
                part = jnp.where(
                    lane_8 == target, pltpu.roll(tiles[slot], (target - at) % LANES, 1), part
                )
            HB[rows, :] = part

    def zm(a):
        return jnp.where(lane_c == 0, 0.0, pltpu.roll(a, 1, 1))

    def zp(a):
        return jnp.where(lane_c == LANES - 1, 0.0, pltpu.roll(a, LANES - 1, 1))

    def unpack(x, a):
        part = pltpu.roll(CP[pl.ds(a, CH), :], lax.rem(LANES - 2 * x, LANES), 1)
        return jnp.where(jnp.logical_or(lane_c == 0, lane_c == LANES - 1), part, 0.0)

    def pack(r, x, a, value):
        to = 2 * x
        other = lax.rem(2 * x + LANES - 1, LANES)
        mask = jnp.logical_or(lane_c == to, lane_c == other)
        rows = pl.ds(a, CH)
        PS[r, rows, :] = jnp.where(mask, pltpu.roll(value, to, 1), PS[r, rows, :])

    scale = (0.5, 0.5, 0.5, 0.25, 0.25, 0.25)
    count = cond.shape[1]
    table = [[cond[c, k] * scale[c] for k in range(count)] for c in range(6)]
    self_row = [cond[6, k] for k in range(count)]

    def lookup(values, components):
        outs = [jnp.zeros(values.shape, f32) for _ in components]
        for k in range(count):
            hit = values == f32(k + 1)
            outs = [
                jnp.where(hit, (self_row if c == 6 else table[c])[k], o)
                for c, o in zip(components, outs)
            ]
        return outs

    PS[...] = jnp.zeros(PS.shape, f32)
    MA[...] = jnp.zeros(MA.shape, f32)
    chunks = [PAD + i for i in range(0, Y, CH)]

    @pl.loop(0, X)
    def _(x):
        for a in chunks:
            value = (lab[x, pl.ds(a - PAD, CH), :] + 1).astype(f32)
            V[0, x + 1, pl.ds(a, CH), :] = value
            pack(0, x, a, value)

    start(0)
    wait(0)

    @pl.loop(0, X + 2)
    def _(x):
        for a in range(0, YE, CH):
            for c, s in enumerate(lookup(V[0, x, pl.ds(a, CH), :], range(6))):
                S[c, x, pl.ds(a, CH), :] = s

    build_halo(0)
    for i, s in enumerate(lookup(HB[...], (2, 4, 5))):
        HS[i] = s
    for i, s in enumerate(lookup(PS[0], (2, 4, 5))):
        PG[i] = s
    CP[...] = HS[0]

    def gather8(value):
        total = value[0:8]
        for i in range(8, CH, 8):
            total = total + value[i : i + 8]
        return total

    @pl.loop(0, X)
    def _(x):
        total = jnp.zeros((8, LANES), f32)
        for a in chunks:
            rows = pl.ds(a, CH)
            own = pl.ds(a - PAD, CH)
            (s6,) = lookup(V[0, x + 1, rows, :], (6,))
            s0, s1, s2 = (S[c, x + 1, rows, :] for c in range(3))
            diag = s6 + 2.0 * (s0 + s1 + s2)
            diag = diag + S[0, x, rows, :] + S[0, x + 2, rows, :]
            diag = diag + S[1, x + 1, pl.ds(a - 1, CH), :] + S[1, x + 1, pl.ds(a + 1, CH), :]
            diag = diag + zm(s2) + zp(s2) + unpack(x, a)
            inverse = 1.0 / diag
            DI[x, own, :] = inverse
            r0 = rhs[x, own, :]
            w = r0 * inverse
            V[1, x + 1, rows, :] = w
            pack(1, x, a, w)
            total = total + gather8(r0 * w)
        MA[0] = MA[0] + total

    for step in range(ITERS):
        r = step + 1
        start(r)
        wait(r)
        build_halo(r)
        sign = jnp.where(even, f32(-1.0), f32(1.0))

        def along_x(a):
            return pltpu.roll(a, LANES - 2, 1) - pltpu.roll(a, 2, 1)

        def along_y(a):
            return pltpu.roll(a, YE - 1, 0) - pltpu.roll(a, 1, 0)

        h = HB[...]
        CP[...] = (PG[0] + HS[0]) * h + sign * (
            PG[1] * along_x(h) + along_x(HS[1] * h) + PG[2] * along_y(h) + along_y(HS[2] * h)
        )
        last = step + 1 == ITERS

        @pl.loop(0, X)
        def _(x):
            odd = jnp.zeros((8, LANES), f32)
            evn = jnp.zeros((8, LANES), f32)
            for a in chunks:
                rows, up, down = pl.ds(a, CH), pl.ds(a + 1, CH), pl.ds(a - 1, CH)
                own = pl.ds(a - PAD, CH)
                v = V[r, x + 1, rows, :]
                vu, vd = V[r, x + 1, up, :], V[r, x + 1, down, :]
                p, pu, pd = V[r, x + 2, rows, :], V[r, x + 2, up, :], V[r, x + 2, down, :]
                m, mu, md = V[r, x, rows, :], V[r, x, up, :], V[r, x, down, :]
                dx = p - m
                dy = vu - vd
                q = S[0, x + 1, rows, :] * (m + p) + S[0, x, rows, :] * m + S[0, x + 2, rows, :] * p
                q = q + S[1, x + 1, rows, :] * (vu + vd)
                q = q + S[1, x + 1, up, :] * vu + S[1, x + 1, down, :] * vd
                q = q + S[3, x + 1, rows, :] * ((pu - pd) - (mu - md))
                q = q + (S[3, x + 2, up, :] * pu - S[3, x + 2, down, :] * pd)
                q = q - (S[3, x, up, :] * mu - S[3, x, down, :] * md)
                s2 = S[2, x + 1, rows, :]
                q = q + s2 * (zp(v) + zm(v))
                q = q + S[4, x + 1, rows, :] * (zp(dx) - zm(dx))
                q = q + S[5, x + 1, rows, :] * (zp(dy) - zm(dy))
                u = s2 * v
                g = S[4, x + 2, rows, :] * p - S[4, x, rows, :] * m
                g = g + S[5, x + 1, up, :] * vu - S[5, x + 1, down, :] * vd
                q = q + zp(u + g) + zm(u - g)
                q = q + unpack(x, a)
                odd = odd + gather8(v * q)
                if not last:
                    w = q * DI[x, own, :]
                    evn = evn + gather8(w * q)
                    V[r + 1, x + 1, rows, :] = w
                    pack(r + 1, x, a, w)
            MA[2 * step + 1] = MA[2 * step + 1] + odd
            if not last:
                MA[2 * step + 2] = MA[2 * step + 2] + evn

    row = lax.broadcasted_iota(jnp.int32, (8, LANES), 0)
    tile = jnp.zeros((8, LANES), f32)
    for k in range(MOMENTS):
        tile = jnp.where(row == k, jnp.sum(MA[k], axis=0, keepdims=True), tile)
    for order, i in enumerate((1, 2, 0)):
        n = sizes[i]
        if n == 1:
            continue
        RS[order] = tile
        copies = []
        for t in range(1, n):
            peer = list(me)
            peer[i] = lax.rem(me[i] + t, n)
            c = pltpu.make_async_remote_copy(
                src_ref=RS.at[order],
                dst_ref=RR.at[order, me[i]],
                send_sem=ar_send.at[order, t],
                recv_sem=ar_recv.at[order, t],
                device_id=tuple(peer),
                device_id_type=pl.DeviceIdType.MESH,
            )
            c.start()
            copies.append(c)
        RR[order, me[i]] = tile
        for c in copies:
            c.wait()
        tile = RR[order, 0]
        for t in range(1, n):
            tile = tile + RR[order, t]

    n0, n1, n2, n3, n4, n5 = (
        jnp.sum(tile[k : k + 1], axis=1, keepdims=True) for k in range(MOMENTS)
    )

    def inverse_of(d):
        return jnp.where(d > 0.0, 1.0 / d, 0.0)

    g00, g01, g02, g12, g22 = n0 - n1, n1 - n2, n2 - n3, n3 - n4, n4 - n5
    i0 = 1.0 / g00
    l1, l2 = g01 * i0, g02 * i0
    i1 = inverse_of(g02 - l1 * g01)
    e = g12 - l2 * g01
    l21 = e * i1
    i2 = inverse_of(g22 - l2 * g02 - l21 * e)
    y1 = n1 - l1 * n0
    y2 = n2 - l2 * n0 - l21 * y1
    c2 = y2 * i2
    c1 = y1 * i1 - l21 * c2
    c0 = n0 * i0 - l1 * c1 - l2 * c2

    @pl.loop(0, X)
    def _(x):
        for a in chunks:
            rows = pl.ds(a, CH)
            out[x, pl.ds(a - PAD, CH), :] = (
                c0 * V[1, x + 1, rows, :] + c1 * V[2, x + 1, rows, :] + c2 * V[3, x + 1, rows, :]
            )

    for r in range(ROUNDS):
        for d in directions:
            pl.when(present(d))(lambda d=d, r=r: copy(d, r).wait_send())


def solution(mesh):
    sizes = tuple(mesh.shape[a] for a in AXES)

    def local(labels, conductivity, right_side):
        X, Y, Z = right_side.shape
        YE = Y + 2 * PAD
        f32 = jnp.float32
        vmem = pltpu.VMEM
        return pl.pallas_call(
            functools.partial(kernel, sizes),
            out_shape=jax.ShapeDtypeStruct((X, Y, Z), f32),
            in_specs=[
                pl.BlockSpec(memory_space=pltpu.VMEM),
                pl.BlockSpec(memory_space=pltpu.SMEM),
                pl.BlockSpec(memory_space=pltpu.VMEM),
            ],
            out_specs=pl.BlockSpec(memory_space=pltpu.VMEM),
            scratch_shapes=[
                vmem((ROUNDS, X + 2, YE, Z), f32),
                vmem((6, X + 2, YE, Z), f32),
                vmem((X, Y, Z), f32),
                vmem((ROUNDS, YE, Z), f32),
                vmem((ROUNDS, 2, YE, Z), f32),
                vmem((ROUNDS, 8, Z), f32),
                vmem((ROUNDS, 4, 8, Z), f32),
                vmem((YE, Z), f32),
                vmem((3, YE, Z), f32),
                vmem((3, YE, Z), f32),
                vmem((YE, Z), f32),
                vmem((MOMENTS, 8, Z), f32),
                vmem((3, 8, Z), f32),
                vmem((3, max(sizes), 8, Z), f32),
                pltpu.SemaphoreType.DMA((ROUNDS, 18)),
                pltpu.SemaphoreType.DMA((ROUNDS, 18)),
                pltpu.SemaphoreType.DMA((3, max(sizes))),
                pltpu.SemaphoreType.DMA((3, max(sizes))),
            ],
            compiler_params=pltpu.CompilerParams(
                has_side_effects=True, vmem_limit_bytes=60 * 1024 * 1024
            ),
        )(labels, conductivity, right_side)

    return jax.shard_map(
        local,
        mesh=mesh,
        in_specs=(P("gx", "gy", "gz"), P(), P("gx", "gy", "gz")),
        out_specs=P("gx", "gy", "gz"),
        check_vma=False,
    )
```

time: 400 us -> 71.8 us (0.18)
  blocking collectives: 123 us -> 0 us
  other arithmetic: 106 us -> 0 us
  local copies, waits for them, and re-layouts: 81.7 us -> 2.31 us
  Pallas kernels: 0 us -> 69.3 us
  starting transfers between devices: 57 us -> 0 us
  waiting for transfers between devices: 20.8 us -> 0 us
  between operations: 10.1 us -> 0.01 us
    psum x3 -> x0, blocking collectives: 123 us -> none  [local(): lax.psum((jnp.sum(residual * precond), jnp.sum(applied * precond)), ('gx'...]
    pallas_call x0 -> x1, Pallas kernels: none -> 69.3 us  [local(): pl.pallas_call(functools.partial(kernel, sizes), out_shape=jax.ShapeDtype...]
    ppermute x24 -> x0, starting transfers between devices: 57 us -> none  [the longest x12 41 us: with_halo(): lax.ppermute(tail, axis, [(i, (i + 1) % count) for i in range(ends)])]
    concatenate x11 -> x0, other arithmetic: 45.8 us -> none  [with_halo(): jnp.concatenate([lax.ppermute(tail, axis, [(i, (i + 1) % count) for i in...]
    slice x18 -> x0, local copies, waits for them, and re-layouts: 45.6 us -> none  [the longest x12 31 us: with_halo(): lax.slice_in_dim(cells, cells.shape[dim] - width, cells.shape[dim], axis=...]
    reduce_sum x4 -> x0, other arithmetic: 25.6 us -> none  [the longest x3 21.8 us: local(): jnp.sum(applied * precond)]
    ppermute x8 -> x0, local copies, waits for them, and re-layouts: 23.4 us -> none  [the longest x4 11.8 us: with_halo(): lax.ppermute(head, axis, [((i + 1) % count, i) for i in range(ends)])]
    div x3 -> x0, other arithmetic: 22.8 us -> none  [the longest x1 13.2 us: local(): precond = residual / diag]
  transfers between devices with their start and end apart: 24 -> 0, of which waited for: 9 -> 0; matrix products, arithmetic and copies ran while one was open for 8% -> 0% of each run, Pallas kernels for 0% -> 0%
where the time goes in v1:
time: 71.8 us; the launch traced here: 71.6 us
  Pallas kernels  69.3 us (97%)
  local copies, waits for them, and re-layouts  2.31 us (3%)
    pallas_call x1, Pallas kernels, local(): pl.pallas_call(functools.partial(kernel, sizes), out_shape=jax.ShapeDtype...  69.3 us
    unnamed x1, local copies, waits for them, and re-layouts  2.31 us

profile of v1, /device:TPU:0, one launch (start us, length us, event | category | flops | bytes accessed | tf_op | source)
XLA Modules:
  0.0 71.6 jit_solution(9877206222381003216)
XLA Ops:
  0.0 69.3 %shard_map.37 = f32[32,64,128]{2,1,0:T(8,128)} custom-call(s32[32,64,128]{2,1,0:T(8,128)} %lab.1, f32[7,8]{1,0:T(8,128)} %cond.1, f32[32,64,128]{2,1,0:T(8,128)} %rhs.1), custom_call_target="tpu_custom_call" | custom-call | tf_op jit(solution)/shard_map/pallas_call | solution.py:345
  69.3 2.3 %copy.5 = f32[32,64,128]{2,1,0:T(8,128)} copy(f32[32,64,128]{2,1,0:T(8,128)} %shard_map.37) | data formatting | bytes 2097152

commit v2 on v1

--- a/solution.py
+++ b/solution.py
@@ -1,4 +1,6 @@
 import functools
+import itertools
+import math
 import jax
 import jax.numpy as jnp
 from jax import lax
@@ -16,10 +18,15 @@
 
 
 def kernel(
-    sizes, lab, cond, rhs, out, V, S, DI, PS, PR, ES, ER, HB, HS, PG, CP, MA, RS, RR,
-    send_sem, recv_sem, ar_send, ar_recv,
+    sizes, lab_hbm, cond, rhs_hbm, out, lab, rhs, V0, V1, V2, V3, S, DI, PS, PR, ES, ER, HB, HS, PG, CP, MA, RS, RR,
+    send_sem, recv_sem, ar_send, ar_recv, in_sem,
 ):
+    V = (V0, V1, V2, V3)
     X, Y, Z = rhs.shape
+    lab_copy = pltpu.make_async_copy(lab_hbm, lab, in_sem.at[0])
+    lab_copy.start()
+    rhs_copy = pltpu.make_async_copy(rhs_hbm, rhs, in_sem.at[1])
+    rhs_copy.start()
     YE = Y + 2 * PAD
     TOP = PAD + Y
     me = [lax.axis_index(a) for a in AXES]
@@ -49,9 +56,9 @@
         rows_to = pl.ds(PAD, Y) if dy == 0 else (pl.ds(0, 8) if dy > 0 else pl.ds(TOP, 8))
         if dz == 0:
             if dx == 0:
-                return V.at[r, pl.ds(1, X), rows_from], V.at[r, pl.ds(1, X), rows_to]
+                return V[r].at[pl.ds(1, X), rows_from], V[r].at[pl.ds(1, X), rows_to]
             fx, tx = (X, 0) if dx > 0 else (1, X + 1)
-            return V.at[r, fx, rows_from], V.at[r, tx, rows_to]
+            return V[r].at[fx, rows_from], V[r].at[tx, rows_to]
         side = 0 if dz > 0 else 1
         if dx == 0:
             return PS.at[r, rows_from], PR.at[r, side, rows_to]
@@ -69,6 +76,35 @@
             device_id=tuple(a + t for a, t in zip(me, d)),
             device_id_type=pl.DeviceIdType.MESH,
         )
+
+    groups = [(0, 1, 2)] if math.prod(sizes) <= 32 else [(0, 1), (2,)]
+
+    def offsets(group):
+        ranges = [range(n) if i in group else (0,) for i, n in enumerate(sizes)]
+        return [t for t in itertools.product(*ranges) if any(t)]
+
+    def partner(t):
+        return tuple(lax.rem(m + k, n) for m, k, n in zip(me, t, sizes))
+
+    barrier = pltpu.get_barrier_semaphore()
+    greeted = 0
+    for group in groups:
+        for t in offsets(group):
+            pl.semaphore_signal(
+                barrier, inc=1, device_id=partner(t), device_id_type=pl.DeviceIdType.MESH
+            )
+            greeted += 1
+    if len(groups) > 1:
+        for d in directions:
+            pl.when(present(d))(
+                lambda d=d: pl.semaphore_signal(
+                    barrier,
+                    inc=1,
+                    device_id=tuple(a + t for a, t in zip(me, d)),
+                    device_id_type=pl.DeviceIdType.MESH,
+                )
+            )
+            greeted = greeted + jnp.where(present(d), 1, 0)
 
     for d in [
         (dx, dy, dz)
@@ -138,12 +174,23 @@
         part = pltpu.roll(CP[pl.ds(a, CH), :], lax.rem(LANES - 2 * x, LANES), 1)
         return jnp.where(jnp.logical_or(lane_c == 0, lane_c == LANES - 1), part, 0.0)
 
-    def pack(r, x, a, value):
-        to = 2 * x
-        other = lax.rem(2 * x + LANES - 1, LANES)
-        mask = jnp.logical_or(lane_c == to, lane_c == other)
-        rows = pl.ds(a, CH)
-        PS[r, rows, :] = jnp.where(mask, pltpu.roll(value, to, 1), PS[r, rows, :])
+    def pack(r):
+        @pl.loop(0, Y // 8)
+        def _(k):
+            rows = pl.ds(pl.multiple_of(PAD + 8 * k, 8), 8)
+            parts = [V[r][x + 1, rows, :] for x in range(X)]
+            width = 1
+            while len(parts) > 1:
+                joined = []
+                for i in range(0, len(parts), 2):
+                    low = parts[i]
+                    if i + 1 < len(parts):
+                        keep = jnp.logical_or(lane_8 <= 2 * width - 2, lane_8 == LANES - 1)
+                        low = jnp.where(keep, low, pltpu.roll(parts[i + 1], 2 * width, 1))
+                    joined.append(low)
+                parts = joined
+                width *= 2
+            PS[r, rows, :] = parts[0]
 
     scale = (0.5, 0.5, 0.5, 0.25, 0.25, 0.25)
     count = cond.shape[1]
@@ -161,6 +208,7 @@
         return outs
 
     PS[...] = jnp.zeros(PS.shape, f32)
+    lab_copy.wait()
     MA[...] = jnp.zeros(MA.shape, f32)
     chunks = [PAD + i for i in range(0, Y, CH)]
 
@@ -168,16 +216,17 @@
     def _(x):
         for a in chunks:
             value = (lab[x, pl.ds(a - PAD, CH), :] + 1).astype(f32)
-            V[0, x + 1, pl.ds(a, CH), :] = value
-            pack(0, x, a, value)
-
+            V[0][x + 1, pl.ds(a, CH), :] = value
+
+    pack(0)
+    pl.semaphore_wait(barrier, greeted)
     start(0)
     wait(0)
 
-    @pl.loop(0, X + 2)
+    @pl.loop(0, X + 2, unroll=2)
     def _(x):
         for a in range(0, YE, CH):
-            for c, s in enumerate(lookup(V[0, x, pl.ds(a, CH), :], range(6))):
+            for c, s in enumerate(lookup(V[0][x, pl.ds(a, CH), :], range(6))):
                 S[c, x, pl.ds(a, CH), :] = s
 
     build_halo(0)
@@ -186,6 +235,7 @@
     for i, s in enumerate(lookup(PS[0], (2, 4, 5))):
         PG[i] = s
     CP[...] = HS[0]
+    rhs_copy.wait()
 
     def gather8(value):
         total = value[0:8]
@@ -193,13 +243,13 @@
             total = total + value[i : i + 8]
         return total
 
-    @pl.loop(0, X)
+    @pl.loop(0, X, unroll=2)
     def _(x):
         total = jnp.zeros((8, LANES), f32)
         for a in chunks:
             rows = pl.ds(a, CH)
             own = pl.ds(a - PAD, CH)
-            (s6,) = lookup(V[0, x + 1, rows, :], (6,))
+            (s6,) = lookup(V[0][x + 1, rows, :], (6,))
             s0, s1, s2 = (S[c, x + 1, rows, :] for c in range(3))
             diag = s6 + 2.0 * (s0 + s1 + s2)
             diag = diag + S[0, x, rows, :] + S[0, x + 2, rows, :]
@@ -209,13 +259,13 @@
             DI[x, own, :] = inverse
             r0 = rhs[x, own, :]
             w = r0 * inverse
-            V[1, x + 1, rows, :] = w
-            pack(1, x, a, w)
+            V[1][x + 1, rows, :] = w
             total = total + gather8(r0 * w)
         MA[0] = MA[0] + total
 
     for step in range(ITERS):
         r = step + 1
+        pack(r)
         start(r)
         wait(r)
         build_halo(r)
@@ -233,17 +283,17 @@
         )
         last = step + 1 == ITERS
 
-        @pl.loop(0, X)
+        @pl.loop(0, X, unroll=2)
         def _(x):
             odd = jnp.zeros((8, LANES), f32)
             evn = jnp.zeros((8, LANES), f32)
             for a in chunks:
                 rows, up, down = pl.ds(a, CH), pl.ds(a + 1, CH), pl.ds(a - 1, CH)
                 own = pl.ds(a - PAD, CH)
-                v = V[r, x + 1, rows, :]
-                vu, vd = V[r, x + 1, up, :], V[r, x + 1, down, :]
-                p, pu, pd = V[r, x + 2, rows, :], V[r, x + 2, up, :], V[r, x + 2, down, :]
-                m, mu, md = V[r, x, rows, :], V[r, x, up, :], V[r, x, down, :]
+                v = V[r][x + 1, rows, :]
+                vu, vd = V[r][x + 1, up, :], V[r][x + 1, down, :]
+                p, pu, pd = V[r][x + 2, rows, :], V[r][x + 2, up, :], V[r][x + 2, down, :]
+                m, mu, md = V[r][x, rows, :], V[r][x, up, :], V[r][x, down, :]
                 dx = p - m
                 dy = vu - vd
                 q = S[0, x + 1, rows, :] * (m + p) + S[0, x, rows, :] * m + S[0, x + 2, rows, :] * p
@@ -265,8 +315,7 @@
                 if not last:
                     w = q * DI[x, own, :]
                     evn = evn + gather8(w * q)
-                    V[r + 1, x + 1, rows, :] = w
-                    pack(r + 1, x, a, w)
+                    V[r + 1][x + 1, rows, :] = w
             MA[2 * step + 1] = MA[2 * step + 1] + odd
             if not last:
                 MA[2 * step + 2] = MA[2 * step + 2] + evn
@@ -275,31 +324,32 @@
     tile = jnp.zeros((8, LANES), f32)
     for k in range(MOMENTS):
         tile = jnp.where(row == k, jnp.sum(MA[k], axis=0, keepdims=True), tile)
-    for order, i in enumerate((1, 2, 0)):
-        n = sizes[i]
-        if n == 1:
-            continue
+    for order, group in enumerate(groups):
+        slot = 0
+        members = 1
+        for i in group:
+            slot = slot * sizes[i] + me[i]
+            members *= sizes[i]
         RS[order] = tile
         copies = []
-        for t in range(1, n):
-            peer = list(me)
-            peer[i] = lax.rem(me[i] + t, n)
+        for index, t in enumerate(offsets(group)):
             c = pltpu.make_async_remote_copy(
                 src_ref=RS.at[order],
-                dst_ref=RR.at[order, me[i]],
-                send_sem=ar_send.at[order, t],
-                recv_sem=ar_recv.at[order, t],
-                device_id=tuple(peer),
+                dst_ref=RR.at[order, slot],
+                send_sem=ar_send.at[order, index],
+                recv_sem=ar_recv.at[order, index],
+                device_id=partner(t),
                 device_id_type=pl.DeviceIdType.MESH,
             )
             c.start()
             copies.append(c)
-        RR[order, me[i]] = tile
+        RR[order, slot] = tile
         for c in copies:
             c.wait()
-        tile = RR[order, 0]
-        for t in range(1, n):
-            tile = tile + RR[order, t]
+        parts = [RR[order, t] for t in range(members)]
+        while len(parts) > 1:
+            parts = [sum(parts[i + 1 : i + 2], parts[i]) for i in range(0, len(parts), 2)]
+        tile = parts[0]
 
     n0, n1, n2, n3, n4, n5 = (
         jnp.sum(tile[k : k + 1], axis=1, keepdims=True) for k in range(MOMENTS)
@@ -326,7 +376,7 @@
         for a in chunks:
             rows = pl.ds(a, CH)
             out[x, pl.ds(a - PAD, CH), :] = (
-                c0 * V[1, x + 1, rows, :] + c1 * V[2, x + 1, rows, :] + c2 * V[3, x + 1, rows, :]
+                c0 * V[1][x + 1, rows, :] + c1 * V[2][x + 1, rows, :] + c2 * V[3][x + 1, rows, :]
             )
 
     for r in range(ROUNDS):
@@ -346,13 +396,18 @@
             functools.partial(kernel, sizes),
             out_shape=jax.ShapeDtypeStruct((X, Y, Z), f32),
             in_specs=[
-                pl.BlockSpec(memory_space=pltpu.VMEM),
+                pl.BlockSpec(memory_space=pl.ANY),
                 pl.BlockSpec(memory_space=pltpu.SMEM),
-                pl.BlockSpec(memory_space=pltpu.VMEM),
+                pl.BlockSpec(memory_space=pl.ANY),
             ],
             out_specs=pl.BlockSpec(memory_space=pltpu.VMEM),
             scratch_shapes=[
-                vmem((ROUNDS, X + 2, YE, Z), f32),
+                vmem((X, Y, Z), jnp.int32),
+                vmem((X, Y, Z), f32),
+                vmem((X + 2, YE, Z), f32),
+                vmem((X + 2, YE, Z), f32),
+                vmem((X + 2, YE, Z), f32),
+                vmem((X + 2, YE, Z), f32),
                 vmem((6, X + 2, YE, Z), f32),
                 vmem((X, Y, Z), f32),
                 vmem((ROUNDS, YE, Z), f32),
@@ -364,15 +419,16 @@
                 vmem((3, YE, Z), f32),
                 vmem((YE, Z), f32),
                 vmem((MOMENTS, 8, Z), f32),
-                vmem((3, 8, Z), f32),
-                vmem((3, max(sizes), 8, Z), f32),
+                vmem((2, 8, Z), f32),
+                vmem((2, 32, 8, Z), f32),
                 pltpu.SemaphoreType.DMA((ROUNDS, 18)),
                 pltpu.SemaphoreType.DMA((ROUNDS, 18)),
-                pltpu.SemaphoreType.DMA((3, max(sizes))),
-                pltpu.SemaphoreType.DMA((3, max(sizes))),
+                pltpu.SemaphoreType.DMA((2, 32)),
+                pltpu.SemaphoreType.DMA((2, 32)),
+                pltpu.SemaphoreType.DMA((2,)),
             ],
             compiler_params=pltpu.CompilerParams(
-                has_side_effects=True, vmem_limit_bytes=60 * 1024 * 1024
+                collective_id=0, has_side_effects=True, vmem_limit_bytes=60 * 1024 * 1024
             ),
         )(labels, conductivity, right_side)
 

time: 71.8 us -> 63.2 us (0.88)
  Pallas kernels: 69.3 us -> 60.7 us
    pallas_call x1, Pallas kernels: 69.3 us -> 60.7 us  [local(): pl.pallas_call(functools.partial(kernel, sizes), out_shape=jax.ShapeDtype...]
where the time goes in v2:
time: 63.2 us; the launch traced here: 63 us
  Pallas kernels  60.7 us (96%)
  local copies, waits for them, and re-layouts  2.31 us (4%)
    pallas_call x1, Pallas kernels, local(): pl.pallas_call(functools.partial(kernel, sizes), out_shape=jax.ShapeDtype...  60.7 us
    unnamed x1, local copies, waits for them, and re-layouts  2.31 us

profile of v2, /device:TPU:0, one launch (start us, length us, event | category | flops | bytes accessed | tf_op | source)
XLA Modules:
  0.0 63.0 jit_solution(12643142984001973010)
XLA Ops:
  0.0 60.7 %shard_map.37 = f32[32,64,128]{2,1,0:T(8,128)} custom-call(s32[32,64,128]{2,1,0:T(8,128)} %lab_hbm.1, f32[7,8]{1,0:T(8,128)} %cond.1, f32[32,64,128]{2,1,0:T(8,128)} %rhs_hbm.1), custom_call_target="tpu_custom_call" | custom-call | tf_op jit(solution)/shard_map/pallas_call | solution.py:395
  60.7 2.3 %copy.5 = f32[32,64,128]{2,1,0:T(8,128)} copy(f32[32,64,128]{2,1,0:T(8,128)} %shard_map.37) | data formatting | bytes 2097152

commit v3 on v2

--- a/solution.py
+++ b/solution.py
@@ -175,7 +175,7 @@
         return jnp.where(jnp.logical_or(lane_c == 0, lane_c == LANES - 1), part, 0.0)
 
     def pack(r):
-        @pl.loop(0, Y // 8)
+        @pl.loop(0, Y // 8, unroll=4)
         def _(k):
             rows = pl.ds(pl.multiple_of(PAD + 8 * k, 8), 8)
             parts = [V[r][x + 1, rows, :] for x in range(X)]
@@ -243,7 +243,7 @@
             total = total + value[i : i + 8]
         return total
 
-    @pl.loop(0, X, unroll=2)
+    @pl.loop(0, X, unroll=4)
     def _(x):
         total = jnp.zeros((8, LANES), f32)
         for a in chunks:
@@ -283,7 +283,7 @@
         )
         last = step + 1 == ITERS
 
-        @pl.loop(0, X, unroll=2)
+        @pl.loop(0, X, unroll=4)
         def _(x):
             odd = jnp.zeros((8, LANES), f32)
             evn = jnp.zeros((8, LANES), f32)

time: 63.2 us -> 53.4 us (0.84)
  Pallas kernels: 60.7 us -> 50.8 us
    pallas_call x1, Pallas kernels: 60.7 us -> 50.8 us  [local(): pl.pallas_call(functools.partial(kernel, sizes), out_shape=jax.ShapeDtype...]
where the time goes in v3:
time: 53.4 us; the launch traced here: 53.2 us
  Pallas kernels  50.8 us (95%)
  local copies, waits for them, and re-layouts  2.31 us (4%)
    pallas_call x1, Pallas kernels, local(): pl.pallas_call(functools.partial(kernel, sizes), out_shape=jax.ShapeDtype...  50.8 us
    unnamed x1, local copies, waits for them, and re-layouts  2.31 us

profile of v3, /device:TPU:0, one launch (start us, length us, event | category | flops | bytes accessed | tf_op | source)
XLA Modules:
  0.0 53.2 jit_solution(4163912555919488606)
XLA Ops:
  0.0 50.8 %shard_map.37 = f32[32,64,128]{2,1,0:T(8,128)} custom-call(s32[32,64,128]{2,1,0:T(8,128)} %lab_hbm.1, f32[7,8]{1,0:T(8,128)} %cond.1, f32[32,64,128]{2,1,0:T(8,128)} %rhs_hbm.1), custom_call_target="tpu_custom_call" | custom-call | tf_op jit(solution)/shard_map/pallas_call | solution.py:395
  50.8 2.3 %copy.5 = f32[32,64,128]{2,1,0:T(8,128)} copy(f32[32,64,128]{2,1,0:T(8,128)} %shard_map.37) | data formatting | bytes 2097152
